TPU v7x, 32 devices: a whole 2x2x4 slice. The times are simulated.
32 devices in a mesh: grp: 4 (over z), loc: 8 (over y, x, core).
Axes of the slice: x: 2, y: 2, z: 4, core: 2. Of those that a mesh axis runs over, the one named last changes fastest.
Arguments:
- features: float32 [32768, 256], P(('grp', 'loc')), may hold values from -6 to 6
- hub_block: bfloat16 [128, 32768], P(None, ('grp', 'loc')), may hold values from -0.0625 to 0.0625
- hub_slot: int32 [128], P(('grp', 'loc')), may hold values from 0 to 1023, as said below
- neighbours: int32 [32768, 16], P(('grp', 'loc')), may hold values from 0 to 2047
- counts: int32 [32768], P(('grp', 'loc')), may hold values from 1 to 16
- halo_send: int32 [256, 128], P(('grp', 'loc')), may hold values from 0 to 1023
- weight: float32 [256, 256], replicated, may hold values from -0.375 to 0.375
- bias: float32 [256], replicated, may hold values from -3 to 3
Outputs:
- layer_out: float32 [32768, 256], P(('grp', 'loc'))
Inputs may be any that keep to these rules, and one draw needn't show every extreme that they name: `hub_slot`: within each aligned block of 4 entries the values are distinct.
All inputs are finite; a program needn't handle non-finite values.
Results may differ from a plain program's by a relative error of at most 0.0003.
Values sent between devices are 32-bit elements; how exact they have to be, the bound alone decides.
A program may use at most 64 MiB of HBM per device.

v0:
```python
import functools

import jax
import jax.numpy as jnp
from jax import lax
from jax.experimental import pallas as pl
from jax.experimental.pallas import tpu as pltpu
from jax.sharding import PartitionSpec as P

BF = jnp.bfloat16
F32 = jnp.float32
LANES = 128


def flip(index, mask, count):
    result = index
    bit = 1
    while bit < count:
        if mask & bit:
            result = result + bit * (1 - 2 * ((index // bit) % 2))
        bit *= 2
    return result


def send_order(count):
    far = [off for off in range(2, count) if bin(off >> 1).count("1") > 1]
    near = [off for off in range(2, count) if bin(off >> 1).count("1") == 1][::-1]
    order = []
    while far or near:
        if far:
            order.append(far.pop(0))
        if near:
            order.append(near.pop(0))
    return order + [1]


def dot(a, b):
    return jnp.dot(a, b, preferred_element_type=F32)


def dot_nt(a, b):
    return lax.dot_general(a, b, (((1,), (1,)), ((), ())), preferred_element_type=F32)


def split(x):
    high = x.astype(BF)
    return high, (x - high.astype(F32)).astype(BF)


def onehot(mask):
    return jnp.where(mask, 1.0, 0.0).astype(BF)


def iota(shape, dim):
    return lax.broadcasted_iota(jnp.int32, shape, dim)


def kernel(
    n_grp, n_loc,
    feat_hbm, hub_hbm, slot_hbm, nbr_hbm, cnt_hbm, halo_hbm, w_hbm, bias_hbm,
    out_ref,
    feat_ref, hub_ref, slot_ref, nbr_ref, cnt_ref, halo_ref, w_ref, bias_ref, loaded,
    fh, fl, ph, pl_, base, acc, adj_own, adj, codes, lows, outgoing, recv, part, part_in, spread, spread_in,
    inv, wh, wl,
    halo_s, halo_r, grp_s, grp_r, loc_s, loc_r,
):
    grp = lax.axis_index("grp")
    me = lax.axis_index("loc")
    rows, width = feat_ref.shape
    listed = halo_ref.shape[1]
    slots = nbr_ref.shape[0]
    hub_grp = hub_ref.shape[0] // n_grp
    hub_dev = slot_ref.shape[0]
    levels = rows // LANES + n_loc * listed // LANES
    per_block = 256 // slots
    blocks = rows // per_block

    barrier = pltpu.get_barrier_semaphore()
    for off in range(1, n_loc):
        pl.semaphore_signal(
            barrier, inc=1, device_id={"loc": flip(me, off, n_loc)}, device_id_type=pl.DeviceIdType.MESH
        )
    for off in range(1, n_grp):
        pl.semaphore_signal(
            barrier, inc=1, device_id={"grp": (grp + off) % n_grp}, device_id_type=pl.DeviceIdType.MESH
        )

    halo_load, feat_load, hub_load, nbr_load, cnt_load, w_load, bias_load, slot_load = [
        pltpu.make_async_copy(source, target, loaded.at[number])
        for number, (source, target) in enumerate((
            (halo_hbm, halo_ref), (feat_hbm, feat_ref), (hub_hbm, hub_ref), (nbr_hbm, nbr_ref),
            (cnt_hbm, cnt_ref), (w_hbm, w_ref), (bias_hbm, bias_ref), (slot_hbm, slot_ref),
        ))
    ]
    for load in (feat_load, w_load, bias_load, halo_load, hub_load, nbr_load, cnt_load, slot_load):
        load.start()
    halo_load.wait()
    feat_load.wait()
    high, low = split(feat_ref[...])
    fh[...] = high
    fl[...] = low

    w_load.wait()
    bias_load.wait()
    w_high, w_low = split(w_ref[...])
    wh[...] = w_high
    wl[...] = w_low

    def times_weight(x_high, x_low):
        return dot(x_high, wh[...]) + dot(x_low, wh[...]) + dot(x_high, wl[...])

    product = times_weight(fh[...], fl[...])
    base[...] = product + bias_ref[...]
    p_high, p_low = split(product)
    ph[...] = p_high
    pl_[...] = p_low

    def gather(peer):
        line = halo_ref[pl.ds(peer, 1), :]
        column = jnp.transpose(jnp.broadcast_to(line, (LANES, listed)).astype(F32)).astype(jnp.int32)
        lane = iota((listed, LANES), 1)
        pick = jnp.concatenate(
            [onehot(column == lane + tile * LANES) for tile in range(rows // LANES)], axis=1
        )
        return dot(pick, ph[...]) + dot(pick, pl_[...])

    def halo_copy(off):
        return pltpu.make_async_remote_copy(
            src_ref=outgoing.at[off],
            dst_ref=recv.at[pl.ds(pl.multiple_of(me * listed, listed), listed)],
            send_sem=halo_s.at[off],
            recv_sem=halo_r.at[off],
            device_id={"loc": flip(me, off, n_loc)},
            device_id_type=pl.DeviceIdType.MESH,
        )

    def grp_copy(off):
        target = (grp + off) % n_grp
        return pltpu.make_async_remote_copy(
            src_ref=part.at[pl.ds(pl.multiple_of(target * hub_grp, hub_grp), hub_grp)],
            dst_ref=part_in.at[off],
            send_sem=grp_s.at[off],
            recv_sem=grp_r.at[off],
            device_id={"grp": target},
            device_id_type=pl.DeviceIdType.MESH,
        )

    def loc_copy(off):
        target = flip(me, off, n_loc)
        return pltpu.make_async_remote_copy(
            src_ref=spread.at[target],
            dst_ref=spread_in.at[off],
            send_sem=loc_s.at[off],
            recv_sem=loc_r.at[off],
            device_id={"loc": target},
            device_id_type=pl.DeviceIdType.MESH,
        )

    order = send_order(n_loc)
    outgoing[order[0]] = gather(flip(me, order[0], n_loc))
    pl.semaphore_wait(barrier, n_loc - 1 + n_grp - 1)
    halo_copy(order[0]).start()
    for number, off in enumerate(order[1:]):
        outgoing[off] = gather(flip(me, off, n_loc))
        halo_copy(off).start()
        if number == 0:
            hub_load.wait()
            part[...] = dot(hub_ref[...], fh[...])
            for grp_off in range(1, n_grp):
                grp_copy(grp_off).start()
    recv[pl.ds(pl.multiple_of(me * listed, listed), listed), :] = gather(me)

    nbr_load.wait()
    cnt_load.wait()
    slot = nbr_ref[...]
    used = iota((slots, rows), 0) < jnp.broadcast_to(cnt_ref[...], (slots, rows))
    level = jnp.where(used, lax.shift_right_logical(slot, 7), -16).astype(F32)
    place = jnp.where(used, slot & (LANES - 1), 0).astype(F32)
    spots = (iota((rows, 256), 0) % per_block) == (iota((rows, 256), 1) % per_block)
    repeat = onehot(iota((slots, 256), 1) // per_block == iota((slots, 256), 0))
    member = onehot(iota((blocks, rows), 1) // per_block == iota((blocks, rows), 0))

    def flatten(table):
        spread_out = dot(jnp.transpose(table).astype(BF), repeat)
        return dot(member, jnp.where(spots, spread_out, 0.0).astype(BF))

    codes[...] = flatten(level).astype(jnp.int32) * per_block + iota((blocks, 256), 1) % per_block
    lows[...] = flatten(place).astype(jnp.int32)
    inv[...] = 1.0 / jnp.transpose(jnp.broadcast_to(cnt_ref[...].astype(F32), (8, rows)))

    group = 4
    own = rows // 256

    def build(step, carry):
        for inner in range(group):
            block = step * group + inner
            code = codes[pl.ds(block, 1), :]
            spot = lows[pl.ds(block, 1), :]
            left = onehot(iota((levels * per_block, 256), 0) == code)
            right = onehot(iota((LANES, 256), 0) == spot)
            counted = dot_nt(left, right).astype(BF)
            at = pl.ds(pl.multiple_of(block * per_block, per_block), per_block)
            for tile in range(levels):
                piece = counted[tile * per_block:(tile + 1) * per_block]
                if tile < 2 * own:
                    adj_own[at, tile * LANES:(tile + 1) * LANES] = piece
                else:
                    adj[tile - 2 * own, at, 0:LANES] = piece
                    adj[tile - 2 * own, at, LANES:2 * LANES] = piece
        return carry

    lax.fori_loop(0, blocks // group, build, 0)

    acc[...] = dot(adj_own[...], ph[...]) + dot(adj_own[...], pl_[...])

    for off in range(1, n_grp):
        grp_copy(off).wait_recv()
    group_sum = part[pl.ds(pl.multiple_of(grp * hub_grp, hub_grp), hub_grp), :]
    for off in range(1, n_grp):
        group_sum = group_sum + part_in[off]
    spread[...] = jnp.zeros_like(spread)
    for owner in range(n_loc):
        spread[owner, 0:hub_dev, :] = group_sum[owner * hub_dev:(owner + 1) * hub_dev]
    for off in range(1, n_loc):
        loc_copy(off).start()

    def take(off):
        peer = flip(me, off, n_loc)
        got = recv[pl.ds(pl.multiple_of(peer * listed, listed), listed), :]
        r_high, r_low = split(got)
        return dot(adj[peer], jnp.concatenate([r_high, r_low], axis=0))

    acc[...] += take(0)
    arrivals = [1] + order[:-1]
    for off in arrivals[:-1]:
        halo_copy(off).wait_recv()
        acc[...] += take(off)

    hubs = spread[me]
    for off in range(1, n_loc):
        loc_copy(off).wait_recv()
        hubs = hubs + spread_in[off]
    hubs = jnp.concatenate([hubs, jnp.zeros((LANES - hubs.shape[0], width), F32)], axis=0)
    h_high, h_low = split(times_weight(*split(hubs)))
    slot_load.wait()
    lane = iota((1, LANES), 1)
    target_row = jnp.full((1, LANES), -1, jnp.int32)
    for hub in range(hub_dev):
        target_row = jnp.where(lane == hub, slot_ref[hub], target_row)
    here = onehot(iota((rows, LANES), 0) == target_row)
    base[...] += dot(here, h_high) + dot(here, h_low)

    last = arrivals[-1]
    halo_copy(last).wait_recv()
    out_ref[...] = jnp.maximum((acc[...] + take(last)) * inv[:, 0:1] + base[...], 0.0)

    for off in range(1, n_loc):
        halo_copy(off).wait_send()
        loc_copy(off).wait_send()
    for off in range(1, n_grp):
        grp_copy(off).wait_send()


def solution(mesh):
    n_grp, n_loc = mesh.shape["grp"], mesh.shape["loc"]

    def on_device(features, hub_block, hub_slot, neighbours, counts, halo_send, weight, bias):
        rows, width = features.shape
        slots = neighbours.shape[1]
        listed = halo_send.shape[1]
        hubs = hub_block.shape[0]
        blocks = rows // (256 // slots)
        padded = -(-hub_slot.shape[0] // 8) * 8
        vmem = pl.BlockSpec(memory_space=pltpu.VMEM)
        far = pl.BlockSpec(memory_space=pltpu.HBM)
        sem = pltpu.SemaphoreType.DMA
        return pl.pallas_call(
            functools.partial(kernel, n_grp, n_loc),
            out_shape=jax.ShapeDtypeStruct((rows, width), F32),
            in_specs=[far] * 8,
            out_specs=vmem,
            scratch_shapes=[
                pltpu.VMEM(features.shape, F32),
                pltpu.VMEM(hub_block.shape, BF),
                pltpu.SMEM(hub_slot.shape, jnp.int32),
                pltpu.VMEM((slots, rows), jnp.int32),
                pltpu.VMEM((1, rows), jnp.int32),
                pltpu.VMEM(halo_send.shape, jnp.int32),
                pltpu.VMEM(weight.shape, F32),
                pltpu.VMEM((1, width), F32),
                sem((8,)),
                pltpu.VMEM((rows, width), BF),
                pltpu.VMEM((rows, width), BF),
                pltpu.VMEM((rows, width), BF),
                pltpu.VMEM((rows, width), BF),
                pltpu.VMEM((rows, width), F32),
                pltpu.VMEM((rows, width), F32),
                pltpu.VMEM((rows, rows), BF),
                pltpu.VMEM((n_loc, rows, 256), BF),
                pltpu.VMEM((blocks, 256), jnp.int32),
                pltpu.VMEM((blocks, 256), jnp.int32),
                pltpu.VMEM((n_loc, listed, width), F32),
                pltpu.VMEM((n_loc * listed, width), F32),
                pltpu.VMEM((hubs, width), F32),
                pltpu.VMEM((n_grp, hubs // n_grp, width), F32),
                pltpu.VMEM((n_loc, padded, width), F32),
                pltpu.VMEM((n_loc, padded, width), F32),
                pltpu.VMEM((rows, 8), F32),
                pltpu.VMEM(weight.shape, BF),
                pltpu.VMEM(weight.shape, BF),
                sem((n_loc,)), sem((n_loc,)), sem((n_grp,)), sem((n_grp,)), sem((n_loc,)), sem((n_loc,)),
            ],
            compiler_params=pltpu.CompilerParams(
                collective_id=0, has_side_effects=True, vmem_limit_bytes=48 * 1024 * 1024
            ),
        )(
            *[
                pltpu.with_memory_space_constraint(array, pltpu.HBM)
                for array in (
                    features, hub_block, hub_slot, neighbours.T, counts.reshape(1, -1), halo_send, weight,
                    bias.reshape(1, -1),
                )
            ]
        )

    both = ("grp", "loc")
    return jax.shard_map(
        on_device,
        mesh=mesh,
        in_specs=(P(both, None), P(None, both), P(both), P(both, None), P(both), P(both, None), P(), P()),
        out_specs=P(both, None),
        check_vma=False,
    )
```

profile of v0, /device:TPU:0, one launch (start us, length us, event | category | flops | bytes accessed | tf_op | source)
XLA Modules:
  0.0 23.9 jit_solution(4384087163581895715)
XLA Ops:
  0.0 22.9 %shard_map.82 = f32[1024,256]{1,0:T(8,128)S(1)} custom-call(f32[1024,256]{1,0:T(8,128)} %feat_hbm.1, bf16[128,1024]{1,0:T(8,128)(2,1)} %hub_hbm.1, s32[4]{0:T(128)} %slot_hbm.1, s32[16,1024]{1,0:T(8,128)} %bitcast.3, s32[1,1024]{1,0:T(1,128)} %bitcast.4, s32[8,128]{1,0:T(8,128)} %halo_hbm.1, f32[256,256]{1,0:T(8,128)} %w_hbm.1, f32[1,256]{1,0:T(1,128)} %bitcast.5), custom_call_target="tpu_custom_call" | custom-call | tf_op jit(solution)/shard_map/pallas_call | solution.py:277
  22.9 1.0 %copy.10 = f32[1024,256]{1,0:T(8,128)} copy(f32[1024,256]{1,0:T(8,128)S(1)} %shard_map.82) | data formatting | bytes 2097152
where the time goes:
time: 24.1 us; the launch traced here: 23.9 us
  Pallas kernels  22.9 us (95%)
  local copies, waits for them, and re-layouts  0.97 us (4%)
    pallas_call x1, Pallas kernels, on_device(): pl.pallas_call(functools.partial(kernel, n_grp, n_loc), out_shape=jax.Sha...  22.9 us
    unnamed x1, local copies, waits for them, and re-layouts  0.97 us

commit v1 on v0

--- a/solution.py
+++ b/solution.py
@@ -23,15 +23,10 @@
 
 
 def send_order(count):
+    near = [off for off in range(2, count) if bin(off >> 1).count("1") == 1]
     far = [off for off in range(2, count) if bin(off >> 1).count("1") > 1]
-    near = [off for off in range(2, count) if bin(off >> 1).count("1") == 1][::-1]
-    order = []
-    while far or near:
-        if far:
-            order.append(far.pop(0))
-        if near:
-            order.append(near.pop(0))
-    return order + [1]
+    near.sort(key=lambda off: (off & 1, off))
+    return near[:2] + [1] + near[2:] + far
 
 
 def dot(a, b):
@@ -60,7 +55,7 @@
     feat_hbm, hub_hbm, slot_hbm, nbr_hbm, cnt_hbm, halo_hbm, w_hbm, bias_hbm,
     out_ref,
     feat_ref, hub_ref, slot_ref, nbr_ref, cnt_ref, halo_ref, w_ref, bias_ref, loaded,
-    fh, fl, ph, pl_, base, acc, adj_own, adj, codes, lows, outgoing, recv, part, part_in, spread, spread_in,
+    go, fh, ph, pl_, prod, base, acc, adj_own, adj, codes, lows, outgoing, recv, part, part_in, spread, spread_in,
     inv, wh, wl,
     halo_s, halo_r, grp_s, grp_r, loc_s, loc_r,
 ):
@@ -80,10 +75,6 @@
         pl.semaphore_signal(
             barrier, inc=1, device_id={"loc": flip(me, off, n_loc)}, device_id_type=pl.DeviceIdType.MESH
         )
-    for off in range(1, n_grp):
-        pl.semaphore_signal(
-            barrier, inc=1, device_id={"grp": (grp + off) % n_grp}, device_id_type=pl.DeviceIdType.MESH
-        )
 
     halo_load, feat_load, hub_load, nbr_load, cnt_load, w_load, bias_load, slot_load = [
         pltpu.make_async_copy(source, target, loaded.at[number])
@@ -92,37 +83,22 @@
             (cnt_hbm, cnt_ref), (w_hbm, w_ref), (bias_hbm, bias_ref), (slot_hbm, slot_ref),
         ))
     ]
-    for load in (feat_load, w_load, bias_load, halo_load, hub_load, nbr_load, cnt_load, slot_load):
+    for load in (halo_load, feat_load, w_load, bias_load, hub_load, nbr_load, cnt_load, slot_load):
         load.start()
-    halo_load.wait()
-    feat_load.wait()
-    high, low = split(feat_ref[...])
-    fh[...] = high
-    fl[...] = low
-
-    w_load.wait()
-    bias_load.wait()
-    w_high, w_low = split(w_ref[...])
-    wh[...] = w_high
-    wl[...] = w_low
 
     def times_weight(x_high, x_low):
         return dot(x_high, wh[...]) + dot(x_low, wh[...]) + dot(x_high, wl[...])
 
-    product = times_weight(fh[...], fl[...])
-    base[...] = product + bias_ref[...]
-    p_high, p_low = split(product)
-    ph[...] = p_high
-    pl_[...] = p_low
-
-    def gather(peer):
-        line = halo_ref[pl.ds(peer, 1), :]
-        column = jnp.transpose(jnp.broadcast_to(line, (LANES, listed)).astype(F32)).astype(jnp.int32)
-        lane = iota((listed, LANES), 1)
-        pick = jnp.concatenate(
-            [onehot(column == lane + tile * LANES) for tile in range(rows // LANES)], axis=1
-        )
-        return dot(pick, ph[...]) + dot(pick, pl_[...])
+    chunk = 16
+
+    def gather(source, peer, target, start):
+        def rows_of(step, carry):
+            for inner in range(chunk):
+                row = step * chunk + inner
+                target[pl.ds(start + row, 1), :] = source[pl.ds(halo_ref[peer, row], 1), :]
+            return carry
+
+        lax.fori_loop(0, listed // chunk, rows_of, 0)
 
     def halo_copy(off):
         return pltpu.make_async_remote_copy(
@@ -157,18 +133,55 @@
         )
 
     order = send_order(n_loc)
-    outgoing[order[0]] = gather(flip(me, order[0], n_loc))
-    pl.semaphore_wait(barrier, n_loc - 1 + n_grp - 1)
-    halo_copy(order[0]).start()
-    for number, off in enumerate(order[1:]):
-        outgoing[off] = gather(flip(me, off, n_loc))
+    early, late, held = order[:2], order[2:-1], order[-1]
+
+    halo_load.wait()
+    feat_load.wait()
+    gather(feat_ref, flip(me, early[0], n_loc), outgoing.at[early[0]], 0)
+
+    pl.semaphore_wait(barrier, n_loc - 1 + jnp.where(me == 1, n_grp - 1, 0))
+
+    @pl.when(me == 0)
+    def _():
+        for off in range(1, n_grp):
+            pl.semaphore_signal(
+                barrier, inc=1, device_id={"grp": (grp + off) % n_grp, "loc": 1},
+                device_id_type=pl.DeviceIdType.MESH,
+            )
+
+    @pl.when(me == 1)
+    def _():
+        for off in range(1, n_loc):
+            pl.semaphore_signal(
+                go, inc=1, device_id={"loc": flip(me, off, n_loc)}, device_id_type=pl.DeviceIdType.MESH
+            )
+        pl.semaphore_signal(go, inc=1)
+
+    halo_copy(early[0]).start()
+    for off in early[1:]:
+        gather(feat_ref, flip(me, off, n_loc), outgoing.at[off], 0)
         halo_copy(off).start()
-        if number == 0:
-            hub_load.wait()
-            part[...] = dot(hub_ref[...], fh[...])
-            for grp_off in range(1, n_grp):
-                grp_copy(grp_off).start()
-    recv[pl.ds(pl.multiple_of(me * listed, listed), listed), :] = gather(me)
+
+    w_load.wait()
+    w_high, w_low = split(w_ref[...])
+    wh[...] = w_high
+    wl[...] = w_low
+    high, low = split(feat_ref[...])
+    fh[...] = high
+    product = times_weight(high, low)
+    prod[...] = product
+    p_high, p_low = split(product)
+    ph[...] = p_high
+    pl_[...] = p_low
+
+    for off in late:
+        gather(prod, flip(me, off, n_loc), outgoing.at[off], 0)
+        halo_copy(off).start()
+    gather(prod, flip(me, held, n_loc), outgoing.at[held], 0)
+    gather(prod, me, recv, pl.multiple_of(me * listed, listed))
+
+    hub_load.wait()
+    part[...] = dot(hub_ref[...], fh[...])
 
     nbr_load.wait()
     cnt_load.wait()
@@ -209,30 +222,40 @@
                     adj[tile - 2 * own, at, LANES:2 * LANES] = piece
         return carry
 
-    lax.fori_loop(0, blocks // group, build, 0)
-
-    acc[...] = dot(adj_own[...], ph[...]) + dot(adj_own[...], pl_[...])
+    half = blocks // group // 2
+    lax.fori_loop(0, half, build, 0)
+    pl.semaphore_wait(go, 1)
+    for off in range(1, n_grp):
+        grp_copy(off).start()
+    lax.fori_loop(half, blocks // group, build, 0)
 
     for off in range(1, n_grp):
         grp_copy(off).wait_recv()
     group_sum = part[pl.ds(pl.multiple_of(grp * hub_grp, hub_grp), hub_grp), :]
     for off in range(1, n_grp):
         group_sum = group_sum + part_in[off]
-    spread[...] = jnp.zeros_like(spread)
+    if 2 * hub_dev < spread.shape[1]:
+        spread[...] = jnp.zeros_like(spread)
     for owner in range(n_loc):
-        spread[owner, 0:hub_dev, :] = group_sum[owner * hub_dev:(owner + 1) * hub_dev]
+        own_rows = group_sum[owner * hub_dev:(owner + 1) * hub_dev]
+        spread[owner, 0:hub_dev, :] = own_rows[:, 0:width // 2]
+        spread[owner, hub_dev:2 * hub_dev, :] = own_rows[:, width // 2:]
     for off in range(1, n_loc):
         loc_copy(off).start()
+    halo_copy(held).start()
+
+    acc[...] = dot(adj_own[...], ph[...]) + dot(adj_own[...], pl_[...])
 
     def take(off):
         peer = flip(me, off, n_loc)
         got = recv[pl.ds(pl.multiple_of(peer * listed, listed), listed), :]
+        if off in early:
+            got = times_weight(*split(got))
         r_high, r_low = split(got)
         return dot(adj[peer], jnp.concatenate([r_high, r_low], axis=0))
 
     acc[...] += take(0)
-    arrivals = [1] + order[:-1]
-    for off in arrivals[:-1]:
+    for off in [1] + early + late[1:]:
         halo_copy(off).wait_recv()
         acc[...] += take(off)
 
@@ -240,19 +263,20 @@
     for off in range(1, n_loc):
         loc_copy(off).wait_recv()
         hubs = hubs + spread_in[off]
-    hubs = jnp.concatenate([hubs, jnp.zeros((LANES - hubs.shape[0], width), F32)], axis=0)
+    hubs = jnp.concatenate([hubs[0:hub_dev], hubs[hub_dev:2 * hub_dev]], axis=1)
+    hubs = jnp.concatenate([hubs, jnp.zeros((LANES - hub_dev, width), F32)], axis=0)
     h_high, h_low = split(times_weight(*split(hubs)))
     slot_load.wait()
+    bias_load.wait()
     lane = iota((1, LANES), 1)
     target_row = jnp.full((1, LANES), -1, jnp.int32)
     for hub in range(hub_dev):
         target_row = jnp.where(lane == hub, slot_ref[hub], target_row)
     here = onehot(iota((rows, LANES), 0) == target_row)
-    base[...] += dot(here, h_high) + dot(here, h_low)
-
-    last = arrivals[-1]
-    halo_copy(last).wait_recv()
-    out_ref[...] = jnp.maximum((acc[...] + take(last)) * inv[:, 0:1] + base[...], 0.0)
+    base[...] = prod[...] + bias_ref[...] + dot(here, h_high) + dot(here, h_low)
+
+    halo_copy(held).wait_recv()
+    out_ref[...] = jnp.maximum((acc[...] + take(held)) * inv[:, 0:1] + base[...], 0.0)
 
     for off in range(1, n_loc):
         halo_copy(off).wait_send()
@@ -270,7 +294,7 @@
         listed = halo_send.shape[1]
         hubs = hub_block.shape[0]
         blocks = rows // (256 // slots)
-        padded = -(-hub_slot.shape[0] // 8) * 8
+        padded = -(-2 * hub_slot.shape[0] // 8) * 8
         vmem = pl.BlockSpec(memory_space=pltpu.VMEM)
         far = pl.BlockSpec(memory_space=pltpu.HBM)
         sem = pltpu.SemaphoreType.DMA
@@ -285,14 +309,15 @@
                 pltpu.SMEM(hub_slot.shape, jnp.int32),
                 pltpu.VMEM((slots, rows), jnp.int32),
                 pltpu.VMEM((1, rows), jnp.int32),
-                pltpu.VMEM(halo_send.shape, jnp.int32),
+                pltpu.SMEM(halo_send.shape, jnp.int32),
                 pltpu.VMEM(weight.shape, F32),
                 pltpu.VMEM((1, width), F32),
                 sem((8,)),
+                pltpu.SemaphoreType.REGULAR,
                 pltpu.VMEM((rows, width), BF),
                 pltpu.VMEM((rows, width), BF),
                 pltpu.VMEM((rows, width), BF),
-                pltpu.VMEM((rows, width), BF),
+                pltpu.VMEM((rows, width), F32),
                 pltpu.VMEM((rows, width), F32),
                 pltpu.VMEM((rows, width), F32),
                 pltpu.VMEM((rows, rows), BF),
@@ -303,8 +328,8 @@
                 pltpu.VMEM((n_loc * listed, width), F32),
                 pltpu.VMEM((hubs, width), F32),
                 pltpu.VMEM((n_grp, hubs // n_grp, width), F32),
-                pltpu.VMEM((n_loc, padded, width), F32),
-                pltpu.VMEM((n_loc, padded, width), F32),
+                pltpu.VMEM((n_loc, padded, width // 2), F32),
+                pltpu.VMEM((n_loc, padded, width // 2), F32),
                 pltpu.VMEM((rows, 8), F32),
                 pltpu.VMEM(weight.shape, BF),
                 pltpu.VMEM(weight.shape, BF),

time: 24.1 us -> 26.3 us (1.091)
  Pallas kernels: 22.9 us -> 24.9 us
    pallas_call x1, Pallas kernels: 22.9 us -> 24.9 us  [on_device(): pl.pallas_call(functools.partial(kernel, n_grp, n_loc), out_shape=jax.Sha...]
where the time goes in v1:
time: 26.3 us; the launch traced here: 25.9 us
  Pallas kernels  24.9 us (95%)
  local copies, waits for them, and re-layouts  0.97 us (4%)
    pallas_call x1, Pallas kernels, on_device(): pl.pallas_call(functools.partial(kernel, n_grp, n_loc), out_shape=jax.Sha...  24.9 us
    unnamed x1, local copies, waits for them, and re-layouts  0.97 us

profile of v1, /device:TPU:0, one launch (start us, length us, event | category | flops | bytes accessed | tf_op | source)
XLA Modules:
  0.0 25.9 jit_solution(3032128385292874110)
XLA Ops:
  0.0 24.9 %shard_map.82 = f32[1024,256]{1,0:T(8,128)S(1)} custom-call(f32[1024,256]{1,0:T(8,128)} %feat_hbm.1, bf16[128,1024]{1,0:T(8,128)(2,1)} %hub_hbm.1, s32[4]{0:T(128)} %slot_hbm.1, s32[16,1024]{1,0:T(8,128)} %bitcast.3, s32[1,1024]{1,0:T(1,128)} %bitcast.4, s32[8,128]{1,0:T(8,128)} %halo_hbm.1, f32[256,256]{1,0:T(8,128)} %w_hbm.1, f32[1,256]{1,0:T(1,128)} %bitcast.5), custom_call_target="tpu_custom_call" | custom-call | tf_op jit(solution)/shard_map/pallas_call | solution.py:301
  24.9 1.0 %copy.10 = f32[1024,256]{1,0:T(8,128)} copy(f32[1024,256]{1,0:T(8,128)S(1)} %shard_map.82) | data formatting | bytes 2097152

commit v2 on v1

--- a/solution.py
+++ b/solution.py
@@ -55,14 +55,15 @@
     feat_hbm, hub_hbm, slot_hbm, nbr_hbm, cnt_hbm, halo_hbm, w_hbm, bias_hbm,
     out_ref,
     feat_ref, hub_ref, slot_ref, nbr_ref, cnt_ref, halo_ref, w_ref, bias_ref, loaded,
-    go, fh, ph, pl_, prod, base, acc, adj_own, adj, codes, lows, outgoing, recv, part, part_in, spread, spread_in,
+    go, fh, ph, pl_, prod, table, base, acc, adj_own, adj, codes, lows, outgoing, recv, part, part_in, spread, spread_in,
     inv, wh, wl,
     halo_s, halo_r, grp_s, grp_r, loc_s, loc_r,
 ):
     grp = lax.axis_index("grp")
     me = lax.axis_index("loc")
-    rows, width = feat_ref.shape
-    listed = halo_ref.shape[1]
+    rows, width = feat_hbm.shape
+    chunk = outgoing.shape[3]
+    listed = outgoing.shape[2] * chunk
     slots = nbr_ref.shape[0]
     hub_grp = hub_ref.shape[0] // n_grp
     hub_dev = slot_ref.shape[0]
@@ -76,26 +77,35 @@
             barrier, inc=1, device_id={"loc": flip(me, off, n_loc)}, device_id_type=pl.DeviceIdType.MESH
         )
 
-    halo_load, feat_load, hub_load, nbr_load, cnt_load, w_load, bias_load, slot_load = [
+    order = send_order(n_loc)
+    early, late, held = order[:2], order[2:-1], order[-1]
+
+    halo_load, left_load, hub_load, nbr_load, cnt_load, w_load, bias_load, slot_load, right_load = [
         pltpu.make_async_copy(source, target, loaded.at[number])
         for number, (source, target) in enumerate((
-            (halo_hbm, halo_ref), (feat_hbm, feat_ref), (hub_hbm, hub_ref), (nbr_hbm, nbr_ref),
+            (halo_hbm, halo_ref), (feat_hbm.at[:, 0:LANES], feat_ref.at[0]), (hub_hbm, hub_ref), (nbr_hbm, nbr_ref),
             (cnt_hbm, cnt_ref), (w_hbm, w_ref), (bias_hbm, bias_ref), (slot_hbm, slot_ref),
+            (feat_hbm.at[:, LANES:], feat_ref.at[1]),
         ))
     ]
-    for load in (halo_load, feat_load, w_load, bias_load, hub_load, nbr_load, cnt_load, slot_load):
+    for load in (halo_load, left_load, right_load, w_load, bias_load, hub_load, nbr_load, cnt_load, slot_load):
         load.start()
 
     def times_weight(x_high, x_low):
         return dot(x_high, wh[...]) + dot(x_low, wh[...]) + dot(x_high, wl[...])
 
-    chunk = 16
-
-    def gather(source, peer, target, start):
+    def whole(ref):
+        return jnp.concatenate([ref[0], ref[1]], axis=1)
+
+    def gather(source, peer, target):
+        first = peer * listed
+
         def rows_of(step, carry):
+            at = first + step * chunk
             for inner in range(chunk):
-                row = step * chunk + inner
-                target[pl.ds(start + row, 1), :] = source[pl.ds(halo_ref[peer, row], 1), :]
+                row = halo_ref[at + inner]
+                for side in range(2):
+                    target[side, step, inner:inner + 1, :] = source[side, pl.ds(row, 1), :]
             return carry
 
         lax.fori_loop(0, listed // chunk, rows_of, 0)
@@ -103,10 +113,20 @@
     def halo_copy(off):
         return pltpu.make_async_remote_copy(
             src_ref=outgoing.at[off],
-            dst_ref=recv.at[pl.ds(pl.multiple_of(me * listed, listed), listed)],
+            dst_ref=recv.at[me],
             send_sem=halo_s.at[off],
             recv_sem=halo_r.at[off],
             device_id={"loc": flip(me, off, n_loc)},
+            device_id_type=pl.DeviceIdType.MESH,
+        )
+
+    def held_copy(side):
+        return pltpu.make_async_remote_copy(
+            src_ref=outgoing.at[held, side],
+            dst_ref=recv.at[me, side],
+            send_sem=halo_s.at[held * (1 - side)],
+            recv_sem=halo_r.at[held * (1 - side)],
+            device_id={"loc": flip(me, held, n_loc)},
             device_id_type=pl.DeviceIdType.MESH,
         )
 
@@ -132,14 +152,17 @@
             device_id_type=pl.DeviceIdType.MESH,
         )
 
-    order = send_order(n_loc)
-    early, late, held = order[:2], order[2:-1], order[-1]
-
     halo_load.wait()
-    feat_load.wait()
-    gather(feat_ref, flip(me, early[0], n_loc), outgoing.at[early[0]], 0)
-
-    pl.semaphore_wait(barrier, n_loc - 1 + jnp.where(me == 1, n_grp - 1, 0))
+    left_load.wait()
+    right_load.wait()
+    for off in early:
+        gather(feat_ref, flip(me, off, n_loc), outgoing.at[off])
+
+    @pl.when(me != 1)
+    def _():
+        pl.semaphore_wait(barrier, n_loc - 1)
+        for off in early:
+            halo_copy(off).start()
 
     @pl.when(me == 0)
     def _():
@@ -149,36 +172,32 @@
                 device_id_type=pl.DeviceIdType.MESH,
             )
 
-    @pl.when(me == 1)
-    def _():
-        for off in range(1, n_loc):
-            pl.semaphore_signal(
-                go, inc=1, device_id={"loc": flip(me, off, n_loc)}, device_id_type=pl.DeviceIdType.MESH
-            )
-        pl.semaphore_signal(go, inc=1)
-
-    halo_copy(early[0]).start()
-    for off in early[1:]:
-        gather(feat_ref, flip(me, off, n_loc), outgoing.at[off], 0)
-        halo_copy(off).start()
-
     w_load.wait()
     w_high, w_low = split(w_ref[...])
     wh[...] = w_high
     wl[...] = w_low
-    high, low = split(feat_ref[...])
+    high, low = split(whole(feat_ref))
     fh[...] = high
     product = times_weight(high, low)
-    prod[...] = product
+    for side in range(2):
+        prod[side] = product[:, side * LANES:(side + 1) * LANES]
     p_high, p_low = split(product)
     ph[...] = p_high
     pl_[...] = p_low
 
-    for off in late:
-        gather(prod, flip(me, off, n_loc), outgoing.at[off], 0)
-        halo_copy(off).start()
-    gather(prod, flip(me, held, n_loc), outgoing.at[held], 0)
-    gather(prod, me, recv, pl.multiple_of(me * listed, listed))
+    for off in late + [held]:
+        gather(prod, flip(me, off, n_loc), outgoing.at[off])
+
+    def send_late():
+        for off in late:
+            halo_copy(off).start()
+        held_copy(0).start()
+
+    @pl.when(me != 1)
+    def _():
+        send_late()
+
+    gather(prod, me, recv.at[me])
 
     hub_load.wait()
     part[...] = dot(hub_ref[...], fh[...])
@@ -187,21 +206,16 @@
     cnt_load.wait()
     slot = nbr_ref[...]
     used = iota((slots, rows), 0) < jnp.broadcast_to(cnt_ref[...], (slots, rows))
-    level = jnp.where(used, lax.shift_right_logical(slot, 7), -16).astype(F32)
-    place = jnp.where(used, slot & (LANES - 1), 0).astype(F32)
-    spots = (iota((rows, 256), 0) % per_block) == (iota((rows, 256), 1) % per_block)
-    repeat = onehot(iota((slots, 256), 1) // per_block == iota((slots, 256), 0))
-    member = onehot(iota((blocks, rows), 1) // per_block == iota((blocks, rows), 0))
-
-    def flatten(table):
-        spread_out = dot(jnp.transpose(table).astype(BF), repeat)
-        return dot(member, jnp.where(spots, spread_out, 0.0).astype(BF))
-
-    codes[...] = flatten(level).astype(jnp.int32) * per_block + iota((blocks, 256), 1) % per_block
-    lows[...] = flatten(place).astype(jnp.int32)
-    inv[...] = 1.0 / jnp.transpose(jnp.broadcast_to(cnt_ref[...].astype(F32), (8, rows)))
-
-    group = 4
+    table[:, 0:slots] = jnp.transpose(jnp.where(used, slot, -1))
+    flat = jnp.concatenate(
+        [table[pl.ds(vertex, blocks, stride=per_block), 0:slots] for vertex in range(per_block)], axis=1
+    )
+    level = jnp.where(flat < 0, -1, lax.shift_right_logical(flat, 7))
+    codes[...] = level * per_block + iota((blocks, 256), 1) // slots
+    lows[...] = flat & (LANES - 1)
+    inv[...] = 1.0 / jnp.transpose(jnp.broadcast_to(cnt_ref[...].astype(F32), (LANES, rows)))
+
+    group = 8
     own = rows // 256
 
     def build(step, carry):
@@ -218,16 +232,30 @@
                 if tile < 2 * own:
                     adj_own[at, tile * LANES:(tile + 1) * LANES] = piece
                 else:
-                    adj[tile - 2 * own, at, 0:LANES] = piece
-                    adj[tile - 2 * own, at, LANES:2 * LANES] = piece
+                    adj[tile - 2 * own, at, :] = piece
         return carry
 
-    half = blocks // group // 2
-    lax.fori_loop(0, half, build, 0)
+    steps = blocks // group
+    lax.fori_loop(0, steps // 4, build, 0)
+
+    @pl.when(me == 1)
+    def _():
+        pl.semaphore_wait(barrier, n_loc - 1 + n_grp - 1)
+        for off in range(1, n_loc):
+            pl.semaphore_signal(
+                go, inc=1, device_id={"loc": flip(me, off, n_loc)}, device_id_type=pl.DeviceIdType.MESH
+            )
+        pl.semaphore_signal(go, inc=1)
+        for off in early:
+            halo_copy(off).start()
+        send_late()
+
+    lax.fori_loop(steps // 4, steps // 2, build, 0)
     pl.semaphore_wait(go, 1)
     for off in range(1, n_grp):
         grp_copy(off).start()
-    lax.fori_loop(half, blocks // group, build, 0)
+    lax.fori_loop(steps // 2, steps, build, 0)
+    acc[...] = dot(adj_own[...], ph[...]) + dot(adj_own[...], pl_[...])
 
     for off in range(1, n_grp):
         grp_copy(off).wait_recv()
@@ -242,17 +270,16 @@
         spread[owner, hub_dev:2 * hub_dev, :] = own_rows[:, width // 2:]
     for off in range(1, n_loc):
         loc_copy(off).start()
-    halo_copy(held).start()
-
-    acc[...] = dot(adj_own[...], ph[...]) + dot(adj_own[...], pl_[...])
+    held_copy(1).start()
 
     def take(off):
         peer = flip(me, off, n_loc)
-        got = recv[pl.ds(pl.multiple_of(peer * listed, listed), listed), :]
+        got = jnp.concatenate([recv[peer, side].reshape(listed, LANES) for side in range(2)], axis=1)
         if off in early:
             got = times_weight(*split(got))
         r_high, r_low = split(got)
-        return dot(adj[peer], jnp.concatenate([r_high, r_low], axis=0))
+        column = adj[peer]
+        return dot(jnp.concatenate([column, column], axis=1), jnp.concatenate([r_high, r_low], axis=0))
 
     acc[...] += take(0)
     for off in [1] + early + late[1:]:
@@ -273,13 +300,24 @@
     for hub in range(hub_dev):
         target_row = jnp.where(lane == hub, slot_ref[hub], target_row)
     here = onehot(iota((rows, LANES), 0) == target_row)
-    base[...] = prod[...] + bias_ref[...] + dot(here, h_high) + dot(here, h_low)
-
-    halo_copy(held).wait_recv()
-    out_ref[...] = jnp.maximum((acc[...] + take(held)) * inv[:, 0:1] + base[...], 0.0)
-
+    hub_rows = dot(here, h_high) + dot(here, h_low)
+    scale = inv[...]
+    base[...] = acc[...] * jnp.concatenate([scale, scale], axis=1) + (whole(prod) + bias_ref[...] + hub_rows)
+
+    column = adj[flip(me, held, n_loc)]
+    column = jnp.concatenate([column, column], axis=1)
+    for side in range(2):
+        lanes = slice(side * LANES, (side + 1) * LANES)
+        held_copy(side).wait_recv()
+        r_high, r_low = split(recv[flip(me, held, n_loc), side].reshape(listed, LANES))
+        last = dot(column, jnp.concatenate([r_high, r_low], axis=0))
+        out_ref[:, lanes] = jnp.maximum(last * inv[...] + base[:, lanes], 0.0)
+
+    for off in order[:-1]:
+        halo_copy(off).wait_send()
+    for side in range(2):
+        held_copy(side).wait_send()
     for off in range(1, n_loc):
-        halo_copy(off).wait_send()
         loc_copy(off).wait_send()
     for off in range(1, n_grp):
         grp_copy(off).wait_send()
@@ -292,6 +330,7 @@
         rows, width = features.shape
         slots = neighbours.shape[1]
         listed = halo_send.shape[1]
+        chunk = 32
         hubs = hub_block.shape[0]
         blocks = rows // (256 // slots)
         padded = -(-2 * hub_slot.shape[0] // 8) * 8
@@ -304,33 +343,34 @@
             in_specs=[far] * 8,
             out_specs=vmem,
             scratch_shapes=[
-                pltpu.VMEM(features.shape, F32),
+                pltpu.VMEM((2, rows, LANES), F32),
                 pltpu.VMEM(hub_block.shape, BF),
                 pltpu.SMEM(hub_slot.shape, jnp.int32),
                 pltpu.VMEM((slots, rows), jnp.int32),
                 pltpu.VMEM((1, rows), jnp.int32),
-                pltpu.SMEM(halo_send.shape, jnp.int32),
+                pltpu.SMEM((halo_send.size,), jnp.int32),
                 pltpu.VMEM(weight.shape, F32),
                 pltpu.VMEM((1, width), F32),
-                sem((8,)),
+                sem((9,)),
                 pltpu.SemaphoreType.REGULAR,
                 pltpu.VMEM((rows, width), BF),
                 pltpu.VMEM((rows, width), BF),
                 pltpu.VMEM((rows, width), BF),
-                pltpu.VMEM((rows, width), F32),
+                pltpu.VMEM((2, rows, LANES), F32),
+                pltpu.VMEM((rows, LANES), jnp.int32),
                 pltpu.VMEM((rows, width), F32),
                 pltpu.VMEM((rows, width), F32),
                 pltpu.VMEM((rows, rows), BF),
-                pltpu.VMEM((n_loc, rows, 256), BF),
+                pltpu.VMEM((n_loc, rows, LANES), BF),
                 pltpu.VMEM((blocks, 256), jnp.int32),
                 pltpu.VMEM((blocks, 256), jnp.int32),
-                pltpu.VMEM((n_loc, listed, width), F32),
-                pltpu.VMEM((n_loc * listed, width), F32),
+                pltpu.VMEM((n_loc, 2, listed // chunk, chunk, LANES), F32),
+                pltpu.VMEM((n_loc, 2, listed // chunk, chunk, LANES), F32),
                 pltpu.VMEM((hubs, width), F32),
                 pltpu.VMEM((n_grp, hubs // n_grp, width), F32),
                 pltpu.VMEM((n_loc, padded, width // 2), F32),
                 pltpu.VMEM((n_loc, padded, width // 2), F32),
-                pltpu.VMEM((rows, 8), F32),
+                pltpu.VMEM((rows, LANES), F32),
                 pltpu.VMEM(weight.shape, BF),
                 pltpu.VMEM(weight.shape, BF),
                 sem((n_loc,)), sem((n_loc,)), sem((n_grp,)), sem((n_grp,)), sem((n_loc,)), sem((n_loc,)),
@@ -342,7 +382,7 @@
             *[
                 pltpu.with_memory_space_constraint(array, pltpu.HBM)
                 for array in (
-                    features, hub_block, hub_slot, neighbours.T, counts.reshape(1, -1), halo_send, weight,
+                    features, hub_block, hub_slot, neighbours.T, counts.reshape(1, -1), halo_send.reshape(-1), weight,
                     bias.reshape(1, -1),
                 )
             ]

time: 26.3 us -> 20.5 us (0.78)
  Pallas kernels: 24.9 us -> 19.3 us
    pallas_call x1, Pallas kernels: 24.9 us -> 19.3 us  [on_device(): pl.pallas_call(functools.partial(kernel, n_grp, n_loc), out_shape=jax.Sha...]
where the time goes in v2:
time: 20.5 us; the launch traced here: 20.3 us
  Pallas kernels  19.3 us (94%)
  local copies, waits for them, and re-layouts  0.97 us (5%)
    pallas_call x1, Pallas kernels, on_device(): pl.pallas_call(functools.partial(kernel, n_grp, n_loc), out_shape=jax.Sha...  19.3 us
    unnamed x1, local copies, waits for them, and re-layouts  0.97 us

profile of v2, /device:TPU:0, one launch (start us, length us, event | category | flops | bytes accessed | tf_op | source)
XLA Modules:
  0.0 20.3 jit_solution(3529945804617860999)
XLA Ops:
  0.0 19.3 %shard_map.82 = f32[1024,256]{1,0:T(8,128)S(1)} custom-call(f32[1024,256]{1,0:T(8,128)} %feat_hbm.1, bf16[128,1024]{1,0:T(8,128)(2,1)} %hub_hbm.1, s32[4]{0:T(128)} %slot_hbm.1, s32[16,1024]{1,0:T(8,128)} %bitcast.4, s32[1,1024]{1,0:T(1,128)} %bitcast.5, s32[1024]{0:T(1024)} %bitcast.6, f32[256,256]{1,0:T(8,128)} %w_hbm.1, f32[1,256]{1,0:T(1,128)} %bitcast.7), custom_call_target="tpu_custom_call" | custom-call | tf_op jit(solution)/shard_map/pallas_call | solution.py:340
  19.3 1.0 %copy.10 = f32[1024,256]{1,0:T(8,128)} copy(f32[1024,256]{1,0:T(8,128)S(1)} %shard_map.82) | data formatting | bytes 2097152

commit v3 on v2

--- a/solution.py
+++ b/solution.py
@@ -55,7 +55,7 @@
     feat_hbm, hub_hbm, slot_hbm, nbr_hbm, cnt_hbm, halo_hbm, w_hbm, bias_hbm,
     out_ref,
     feat_ref, hub_ref, slot_ref, nbr_ref, cnt_ref, halo_ref, w_ref, bias_ref, loaded,
-    go, fh, ph, pl_, prod, table, base, acc, adj_own, adj, codes, lows, outgoing, recv, part, part_in, spread, spread_in,
+    near, go, fh, ph, pl_, prod, table, base, acc, adj_own, adj, codes, lows, outgoing, recv, part, part_in, spread, spread_in,
     inv, wh, wl,
     halo_s, halo_r, grp_s, grp_r, loc_s, loc_r,
 ):
@@ -88,7 +88,7 @@
             (feat_hbm.at[:, LANES:], feat_ref.at[1]),
         ))
     ]
-    for load in (halo_load, left_load, right_load, w_load, bias_load, hub_load, nbr_load, cnt_load, slot_load):
+    for load in (halo_load, left_load, right_load, w_load, nbr_load, cnt_load):
         load.start()
 
     def times_weight(x_high, x_low):
@@ -152,25 +152,41 @@
             device_id_type=pl.DeviceIdType.MESH,
         )
 
+    word = n_loc - 1
+
+    @pl.when(me == word - 1)
+    def _():
+        pl.semaphore_wait(barrier, n_loc - 1)
+        pl.semaphore_signal(near, inc=1, device_id={"loc": word}, device_id_type=pl.DeviceIdType.MESH)
+        for off in range(1, n_grp):
+            pl.semaphore_signal(
+                barrier, inc=1, device_id={"grp": (grp + off) % n_grp, "loc": word},
+                device_id_type=pl.DeviceIdType.MESH,
+            )
+
     halo_load.wait()
     left_load.wait()
     right_load.wait()
     for off in early:
         gather(feat_ref, flip(me, off, n_loc), outgoing.at[off])
 
-    @pl.when(me != 1)
+    @pl.when(jnp.logical_and(me > 1, me < word - 1))
     def _():
         pl.semaphore_wait(barrier, n_loc - 1)
-        for off in early:
-            halo_copy(off).start()
-
-    @pl.when(me == 0)
+
+    @pl.when(me == word)
     def _():
-        for off in range(1, n_grp):
-            pl.semaphore_signal(
-                barrier, inc=1, device_id={"grp": (grp + off) % n_grp, "loc": 1},
-                device_id_type=pl.DeviceIdType.MESH,
-            )
+        pl.semaphore_wait(near, 1)
+
+    def send_early(when):
+        @pl.when(when)
+        def _():
+            for off in early:
+                halo_copy(off).start()
+
+    send_early(me > 1)
+    for load in (hub_load, bias_load, slot_load):
+        load.start()
 
     w_load.wait()
     w_high, w_low = split(w_ref[...])
@@ -185,23 +201,6 @@
     ph[...] = p_high
     pl_[...] = p_low
 
-    for off in late + [held]:
-        gather(prod, flip(me, off, n_loc), outgoing.at[off])
-
-    def send_late():
-        for off in late:
-            halo_copy(off).start()
-        held_copy(0).start()
-
-    @pl.when(me != 1)
-    def _():
-        send_late()
-
-    gather(prod, me, recv.at[me])
-
-    hub_load.wait()
-    part[...] = dot(hub_ref[...], fh[...])
-
     nbr_load.wait()
     cnt_load.wait()
     slot = nbr_ref[...]
@@ -214,6 +213,30 @@
     codes[...] = level * per_block + iota((blocks, 256), 1) // slots
     lows[...] = flat & (LANES - 1)
     inv[...] = 1.0 / jnp.transpose(jnp.broadcast_to(cnt_ref[...].astype(F32), (LANES, rows)))
+
+    @pl.when(me <= 1)
+    def _():
+        pl.semaphore_wait(barrier, n_loc - 1)
+
+    send_early(me <= 1)
+
+    for off in late:
+        gather(prod, flip(me, off, n_loc), outgoing.at[off])
+        halo_copy(off).start()
+    gather(prod, flip(me, held, n_loc), outgoing.at[held])
+    gather(prod, me, recv.at[me])
+
+    @pl.when(me == word)
+    def _():
+        pl.semaphore_wait(barrier, n_loc - 1 + n_grp - 1)
+        for off in range(1, n_loc):
+            pl.semaphore_signal(
+                go, inc=1, device_id={"loc": flip(me, off, n_loc)}, device_id_type=pl.DeviceIdType.MESH
+            )
+        pl.semaphore_signal(go, inc=1)
+
+    hub_load.wait()
+    part[...] = dot(hub_ref[...], fh[...])
 
     group = 8
     own = rows // 256
@@ -237,24 +260,10 @@
 
     steps = blocks // group
     lax.fori_loop(0, steps // 4, build, 0)
-
-    @pl.when(me == 1)
-    def _():
-        pl.semaphore_wait(barrier, n_loc - 1 + n_grp - 1)
-        for off in range(1, n_loc):
-            pl.semaphore_signal(
-                go, inc=1, device_id={"loc": flip(me, off, n_loc)}, device_id_type=pl.DeviceIdType.MESH
-            )
-        pl.semaphore_signal(go, inc=1)
-        for off in early:
-            halo_copy(off).start()
-        send_late()
-
-    lax.fori_loop(steps // 4, steps // 2, build, 0)
     pl.semaphore_wait(go, 1)
     for off in range(1, n_grp):
         grp_copy(off).start()
-    lax.fori_loop(steps // 2, steps, build, 0)
+    lax.fori_loop(steps // 4, steps, build, 0)
     acc[...] = dot(adj_own[...], ph[...]) + dot(adj_own[...], pl_[...])
 
     for off in range(1, n_grp):
@@ -262,6 +271,7 @@
     group_sum = part[pl.ds(pl.multiple_of(grp * hub_grp, hub_grp), hub_grp), :]
     for off in range(1, n_grp):
         group_sum = group_sum + part_in[off]
+    group_sum = times_weight(*split(group_sum))
     if 2 * hub_dev < spread.shape[1]:
         spread[...] = jnp.zeros_like(spread)
     for owner in range(n_loc):
@@ -270,7 +280,8 @@
         spread[owner, hub_dev:2 * hub_dev, :] = own_rows[:, width // 2:]
     for off in range(1, n_loc):
         loc_copy(off).start()
-    held_copy(1).start()
+    for side in range(2):
+        held_copy(side).start()
 
     def take(off):
         peer = flip(me, off, n_loc)
@@ -281,18 +292,6 @@
         column = adj[peer]
         return dot(jnp.concatenate([column, column], axis=1), jnp.concatenate([r_high, r_low], axis=0))
 
-    acc[...] += take(0)
-    for off in [1] + early + late[1:]:
-        halo_copy(off).wait_recv()
-        acc[...] += take(off)
-
-    hubs = spread[me]
-    for off in range(1, n_loc):
-        loc_copy(off).wait_recv()
-        hubs = hubs + spread_in[off]
-    hubs = jnp.concatenate([hubs[0:hub_dev], hubs[hub_dev:2 * hub_dev]], axis=1)
-    hubs = jnp.concatenate([hubs, jnp.zeros((LANES - hub_dev, width), F32)], axis=0)
-    h_high, h_low = split(times_weight(*split(hubs)))
     slot_load.wait()
     bias_load.wait()
     lane = iota((1, LANES), 1)
@@ -300,9 +299,22 @@
     for hub in range(hub_dev):
         target_row = jnp.where(lane == hub, slot_ref[hub], target_row)
     here = onehot(iota((rows, LANES), 0) == target_row)
-    hub_rows = dot(here, h_high) + dot(here, h_low)
+
+    acc[...] += take(0)
+    for off in [1] + early + late[1:]:
+        halo_copy(off).wait_recv()
+        acc[...] += take(off)
+
     scale = inv[...]
-    base[...] = acc[...] * jnp.concatenate([scale, scale], axis=1) + (whole(prod) + bias_ref[...] + hub_rows)
+    base[...] = acc[...] * jnp.concatenate([scale, scale], axis=1) + (whole(prod) + bias_ref[...])
+
+    hubs = spread[me]
+    for off in range(1, n_loc):
+        loc_copy(off).wait_recv()
+        hubs = hubs + spread_in[off]
+    hubs = jnp.concatenate([hubs[0:hub_dev], hubs[hub_dev:2 * hub_dev]], axis=1)
+    hubs = jnp.concatenate([hubs, jnp.zeros((LANES - hub_dev, width), F32)], axis=0)
+    base[...] += dot(jnp.concatenate([here, here], axis=1), jnp.concatenate(split(hubs), axis=0))
 
     column = adj[flip(me, held, n_loc)]
     column = jnp.concatenate([column, column], axis=1)
@@ -352,6 +364,7 @@
                 pltpu.VMEM(weight.shape, F32),
                 pltpu.VMEM((1, width), F32),
                 sem((9,)),
+                pltpu.SemaphoreType.REGULAR,
                 pltpu.SemaphoreType.REGULAR,
                 pltpu.VMEM((rows, width), BF),
                 pltpu.VMEM((rows, width), BF),

time: 20.5 us -> 19.4 us (0.946)
  Pallas kernels: 19.3 us -> 18.3 us
    pallas_call x1, Pallas kernels: 19.3 us -> 18.3 us  [on_device(): pl.pallas_call(functools.partial(kernel, n_grp, n_loc), out_shape=jax.Sha...]
where the time goes in v3:
time: 19.4 us; the launch traced here: 19.2 us
  Pallas kernels  18.3 us (94%)
  local copies, waits for them, and re-layouts  0.97 us (5%)
    pallas_call x1, Pallas kernels, on_device(): pl.pallas_call(functools.partial(kernel, n_grp, n_loc), out_shape=jax.Sha...  18.3 us
    unnamed x1, local copies, waits for them, and re-layouts  0.97 us

profile of v3, /device:TPU:0, one launch (start us, length us, event | category | flops | bytes accessed | tf_op | source)
XLA Modules:
  0.0 19.2 jit_solution(8058829260554648416)
XLA Ops:
  0.0 18.3 %shard_map.82 = f32[1024,256]{1,0:T(8,128)S(1)} custom-call(f32[1024,256]{1,0:T(8,128)} %feat_hbm.1, bf16[128,1024]{1,0:T(8,128)(2,1)} %hub_hbm.1, s32[4]{0:T(128)} %slot_hbm.1, s32[16,1024]{1,0:T(8,128)} %bitcast.4, s32[1,1024]{1,0:T(1,128)} %bitcast.5, s32[1024]{0:T(1024)} %bitcast.6, f32[256,256]{1,0:T(8,128)} %w_hbm.1, f32[1,256]{1,0:T(1,128)} %bitcast.7), custom_call_target="tpu_custom_call" | custom-call | tf_op jit(solution)/shard_map/pallas_call | solution.py:352
  18.3 1.0 %copy.10 = f32[1024,256]{1,0:T(8,128)} copy(f32[1024,256]{1,0:T(8,128)S(1)} %shard_map.82) | data formatting | bytes 2097152

commit v4 on v3

--- a/solution.py
+++ b/solution.py
@@ -71,10 +71,10 @@
     per_block = 256 // slots
     blocks = rows // per_block
 
-    barrier = pltpu.get_barrier_semaphore()
-    for off in range(1, n_loc):
-        pl.semaphore_signal(
-            barrier, inc=1, device_id={"loc": flip(me, off, n_loc)}, device_id_type=pl.DeviceIdType.MESH
+    def all_of(ref, count, send_sem, recv_sem):
+        return pltpu.make_async_remote_copy(
+            src_ref=ref.at[0:count], dst_ref=ref.at[0:count], send_sem=send_sem, recv_sem=recv_sem,
+            device_id={"loc": flip(me, 1, n_loc)}, device_id_type=pl.DeviceIdType.MESH,
         )
 
     order = send_order(n_loc)
@@ -91,6 +91,13 @@
     for load in (halo_load, left_load, right_load, w_load, nbr_load, cnt_load):
         load.start()
 
+    barrier = pltpu.get_barrier_semaphore()
+    for off in range(1, n_loc):
+        pl.semaphore_signal(
+            barrier, inc=1, device_id={"loc": flip(me, off, n_loc)}, device_id_type=pl.DeviceIdType.MESH
+        )
+
+
     def times_weight(x_high, x_low):
         return dot(x_high, wh[...]) + dot(x_low, wh[...]) + dot(x_high, wl[...])
 
@@ -135,8 +142,8 @@
         return pltpu.make_async_remote_copy(
             src_ref=part.at[pl.ds(pl.multiple_of(target * hub_grp, hub_grp), hub_grp)],
             dst_ref=part_in.at[off],
-            send_sem=grp_s.at[off],
-            recv_sem=grp_r.at[off],
+            send_sem=grp_s,
+            recv_sem=grp_r,
             device_id={"grp": target},
             device_id_type=pl.DeviceIdType.MESH,
         )
@@ -146,8 +153,8 @@
         return pltpu.make_async_remote_copy(
             src_ref=spread.at[target],
             dst_ref=spread_in.at[off],
-            send_sem=loc_s.at[off],
-            recv_sem=loc_r.at[off],
+            send_sem=loc_s,
+            recv_sem=loc_r,
             device_id={"loc": target},
             device_id_type=pl.DeviceIdType.MESH,
         )
@@ -167,8 +174,8 @@
     halo_load.wait()
     left_load.wait()
     right_load.wait()
-    for off in early:
-        gather(feat_ref, flip(me, off, n_loc), outgoing.at[off])
+    first, second = early
+    gather(feat_ref, flip(me, first, n_loc), outgoing.at[first])
 
     @pl.when(jnp.logical_and(me > 1, me < word - 1))
     def _():
@@ -178,13 +185,14 @@
     def _():
         pl.semaphore_wait(near, 1)
 
-    def send_early(when):
+    def send_early(off, when):
         @pl.when(when)
         def _():
-            for off in early:
-                halo_copy(off).start()
-
-    send_early(me > 1)
+            halo_copy(off).start()
+
+    send_early(first, me > 1)
+    gather(feat_ref, flip(me, second, n_loc), outgoing.at[second])
+    send_early(second, me > 1)
     for load in (hub_load, bias_load, slot_load):
         load.start()
 
@@ -201,6 +209,13 @@
     ph[...] = p_high
     pl_[...] = p_low
 
+    @pl.when(me <= 1)
+    def _():
+        pl.semaphore_wait(barrier, n_loc - 1)
+
+    for off in early:
+        send_early(off, me <= 1)
+
     nbr_load.wait()
     cnt_load.wait()
     slot = nbr_ref[...]
@@ -213,12 +228,6 @@
     codes[...] = level * per_block + iota((blocks, 256), 1) // slots
     lows[...] = flat & (LANES - 1)
     inv[...] = 1.0 / jnp.transpose(jnp.broadcast_to(cnt_ref[...].astype(F32), (LANES, rows)))
-
-    @pl.when(me <= 1)
-    def _():
-        pl.semaphore_wait(barrier, n_loc - 1)
-
-    send_early(me <= 1)
 
     for off in late:
         gather(prod, flip(me, off, n_loc), outgoing.at[off])
@@ -266,8 +275,7 @@
     lax.fori_loop(steps // 4, steps, build, 0)
     acc[...] = dot(adj_own[...], ph[...]) + dot(adj_own[...], pl_[...])
 
-    for off in range(1, n_grp):
-        grp_copy(off).wait_recv()
+    all_of(part_in, n_grp - 1, grp_s, grp_r).wait_recv()
     group_sum = part[pl.ds(pl.multiple_of(grp * hub_grp, hub_grp), hub_grp), :]
     for off in range(1, n_grp):
         group_sum = group_sum + part_in[off]
@@ -309,30 +317,30 @@
     base[...] = acc[...] * jnp.concatenate([scale, scale], axis=1) + (whole(prod) + bias_ref[...])
 
     hubs = spread[me]
+    all_of(spread_in, n_loc - 1, loc_s, loc_r).wait_recv()
     for off in range(1, n_loc):
-        loc_copy(off).wait_recv()
         hubs = hubs + spread_in[off]
     hubs = jnp.concatenate([hubs[0:hub_dev], hubs[hub_dev:2 * hub_dev]], axis=1)
     hubs = jnp.concatenate([hubs, jnp.zeros((LANES - hub_dev, width), F32)], axis=0)
     base[...] += dot(jnp.concatenate([here, here], axis=1), jnp.concatenate(split(hubs), axis=0))
 
-    column = adj[flip(me, held, n_loc)]
-    column = jnp.concatenate([column, column], axis=1)
+    peer = flip(me, held, n_loc)
+    parts = [slice(part * rows // 2, (part + 1) * rows // 2) for part in range(2)]
     for side in range(2):
         lanes = slice(side * LANES, (side + 1) * LANES)
         held_copy(side).wait_recv()
-        r_high, r_low = split(recv[flip(me, held, n_loc), side].reshape(listed, LANES))
-        last = dot(column, jnp.concatenate([r_high, r_low], axis=0))
-        out_ref[:, lanes] = jnp.maximum(last * inv[...] + base[:, lanes], 0.0)
+        pair = jnp.concatenate(split(recv[peer, side].reshape(listed, LANES)), axis=0)
+        for at in parts:
+            column = adj[peer, at, :]
+            last = dot(jnp.concatenate([column, column], axis=1), pair)
+            out_ref[at, lanes] = jnp.maximum(last * inv[at, :] + base[at, lanes], 0.0)
 
     for off in order[:-1]:
         halo_copy(off).wait_send()
     for side in range(2):
         held_copy(side).wait_send()
-    for off in range(1, n_loc):
-        loc_copy(off).wait_send()
-    for off in range(1, n_grp):
-        grp_copy(off).wait_send()
+    all_of(spread_in, n_loc - 1, loc_s, loc_r).wait_send()
+    all_of(part_in, n_grp - 1, grp_s, grp_r).wait_send()
 
 
 def solution(mesh):
@@ -386,7 +394,7 @@
                 pltpu.VMEM((rows, LANES), F32),
                 pltpu.VMEM(weight.shape, BF),
                 pltpu.VMEM(weight.shape, BF),
-                sem((n_loc,)), sem((n_loc,)), sem((n_grp,)), sem((n_grp,)), sem((n_loc,)), sem((n_loc,)),
+                sem((n_loc,)), sem((n_loc,)), sem, sem, sem, sem,
             ],
             compiler_params=pltpu.CompilerParams(
                 collective_id=0, has_side_effects=True, vmem_limit_bytes=48 * 1024 * 1024

time: 19.4 us -> 19.2 us (0.990)
  Pallas kernels: 18.3 us -> 18 us
    pallas_call x1, Pallas kernels: 18.3 us -> 18 us  [on_device(): pl.pallas_call(functools.partial(kernel, n_grp, n_loc), out_shape=jax.Sha...]
where the time goes in v4:
time: 19.2 us; the launch traced here: 19 us
  Pallas kernels  18 us (94%)
  local copies, waits for them, and re-layouts  0.97 us (5%)
    pallas_call x1, Pallas kernels, on_device(): pl.pallas_call(functools.partial(kernel, n_grp, n_loc), out_shape=jax.Sha...  18 us
    unnamed x1, local copies, waits for them, and re-layouts  0.97 us

profile of v4, /device:TPU:0, one launch (start us, length us, event | category | flops | bytes accessed | tf_op | source)
XLA Modules:
  0.0 19.0 jit_solution(15186500664972572313)
XLA Ops:
  0.0 18.0 %shard_map.82 = f32[1024,256]{1,0:T(8,128)S(1)} custom-call(f32[1024,256]{1,0:T(8,128)} %feat_hbm.1, bf16[128,1024]{1,0:T(8,128)(2,1)} %hub_hbm.1, s32[4]{0:T(128)} %slot_hbm.1, s32[16,1024]{1,0:T(8,128)} %bitcast.4, s32[1,1024]{1,0:T(1,128)} %bitcast.5, s32[1024]{0:T(1024)} %bitcast.6, f32[256,256]{1,0:T(8,128)} %w_hbm.1, f32[1,256]{1,0:T(1,128)} %bitcast.7), custom_call_target="tpu_custom_call" | custom-call | tf_op jit(solution)/shard_map/pallas_call | solution.py:360
  18.1 1.0 %copy.10 = f32[1024,256]{1,0:T(8,128)} copy(f32[1024,256]{1,0:T(8,128)S(1)} %shard_map.82) | data formatting | bytes 2097152

commit v5 on v4

--- a/solution.py
+++ b/solution.py
@@ -55,9 +55,9 @@
     feat_hbm, hub_hbm, slot_hbm, nbr_hbm, cnt_hbm, halo_hbm, w_hbm, bias_hbm,
     out_ref,
     feat_ref, hub_ref, slot_ref, nbr_ref, cnt_ref, halo_ref, w_ref, bias_ref, loaded,
-    near, go, fh, ph, pl_, prod, table, base, acc, adj_own, adj, codes, lows, outgoing, recv, part, part_in, spread, spread_in,
+    near, go, fh, ph, pl_, prod, table, base, acc, adj_own, adj, codes, lows, outgoing, recv, mine, pair_in, part, part_in, spread, spread_in,
     inv, wh, wl,
-    halo_s, halo_r, grp_s, grp_r, loc_s, loc_r,
+    halo_s, halo_r, pair_s, pair_r, grp_s, grp_r, loc_s, loc_r,
 ):
     grp = lax.axis_index("grp")
     me = lax.axis_index("loc")
@@ -65,7 +65,6 @@
     chunk = outgoing.shape[3]
     listed = outgoing.shape[2] * chunk
     slots = nbr_ref.shape[0]
-    hub_grp = hub_ref.shape[0] // n_grp
     hub_dev = slot_ref.shape[0]
     levels = rows // LANES + n_loc * listed // LANES
     per_block = 256 // slots
@@ -137,10 +136,16 @@
             device_id_type=pl.DeviceIdType.MESH,
         )
 
+    core = me % 2
+    pair_copy = pltpu.make_async_remote_copy(
+        src_ref=mine.at[1 - core], dst_ref=pair_in, send_sem=pair_s, recv_sem=pair_r,
+        device_id={"loc": flip(me, 1, n_loc)}, device_id_type=pl.DeviceIdType.MESH,
+    )
+
     def grp_copy(off):
         target = (grp + off) % n_grp
         return pltpu.make_async_remote_copy(
-            src_ref=part.at[pl.ds(pl.multiple_of(target * hub_grp, hub_grp), hub_grp)],
+            src_ref=part.at[target],
             dst_ref=part_in.at[off],
             send_sem=grp_s,
             recv_sem=grp_r,
@@ -151,8 +156,8 @@
     def loc_copy(off):
         target = flip(me, off, n_loc)
         return pltpu.make_async_remote_copy(
-            src_ref=spread.at[target],
-            dst_ref=spread_in.at[off],
+            src_ref=spread.at[target // 2],
+            dst_ref=spread_in.at[off // 2],
             send_sem=loc_s,
             recv_sem=loc_r,
             device_id={"loc": target},
@@ -235,6 +240,14 @@
     gather(prod, flip(me, held, n_loc), outgoing.at[held])
     gather(prod, me, recv.at[me])
 
+    hub_load.wait()
+    product = dot(hub_ref[...], fh[...])
+    for side in range(2):
+        mine[side] = jnp.concatenate(
+            [product[owner * hub_dev:(owner + 1) * hub_dev] for owner in range(side, n_grp * n_loc, 2)], axis=0
+        )
+    pair_copy.start()
+
     @pl.when(me == word)
     def _():
         pl.semaphore_wait(barrier, n_loc - 1 + n_grp - 1)
@@ -244,8 +257,6 @@
             )
         pl.semaphore_signal(go, inc=1)
 
-    hub_load.wait()
-    part[...] = dot(hub_ref[...], fh[...])
 
     group = 8
     own = rows // 256
@@ -269,6 +280,8 @@
 
     steps = blocks // group
     lax.fori_loop(0, steps // 4, build, 0)
+    pair_copy.wait_recv()
+    part[...] = (mine[core] + pair_in[...]).reshape(part.shape)
     pl.semaphore_wait(go, 1)
     for off in range(1, n_grp):
         grp_copy(off).start()
@@ -276,17 +289,17 @@
     acc[...] = dot(adj_own[...], ph[...]) + dot(adj_own[...], pl_[...])
 
     all_of(part_in, n_grp - 1, grp_s, grp_r).wait_recv()
-    group_sum = part[pl.ds(pl.multiple_of(grp * hub_grp, hub_grp), hub_grp), :]
+    group_sum = part[grp]
     for off in range(1, n_grp):
         group_sum = group_sum + part_in[off]
     group_sum = times_weight(*split(group_sum))
     if 2 * hub_dev < spread.shape[1]:
         spread[...] = jnp.zeros_like(spread)
-    for owner in range(n_loc):
+    for owner in range(n_loc // 2):
         own_rows = group_sum[owner * hub_dev:(owner + 1) * hub_dev]
         spread[owner, 0:hub_dev, :] = own_rows[:, 0:width // 2]
         spread[owner, hub_dev:2 * hub_dev, :] = own_rows[:, width // 2:]
-    for off in range(1, n_loc):
+    for off in range(2, n_loc, 2):
         loc_copy(off).start()
     for side in range(2):
         held_copy(side).start()
@@ -316,10 +329,10 @@
     scale = inv[...]
     base[...] = acc[...] * jnp.concatenate([scale, scale], axis=1) + (whole(prod) + bias_ref[...])
 
-    hubs = spread[me]
-    all_of(spread_in, n_loc - 1, loc_s, loc_r).wait_recv()
-    for off in range(1, n_loc):
-        hubs = hubs + spread_in[off]
+    hubs = spread[me // 2]
+    all_of(spread_in, n_loc // 2 - 1, loc_s, loc_r).wait_recv()
+    for off in range(2, n_loc, 2):
+        hubs = hubs + spread_in[off // 2]
     hubs = jnp.concatenate([hubs[0:hub_dev], hubs[hub_dev:2 * hub_dev]], axis=1)
     hubs = jnp.concatenate([hubs, jnp.zeros((LANES - hub_dev, width), F32)], axis=0)
     base[...] += dot(jnp.concatenate([here, here], axis=1), jnp.concatenate(split(hubs), axis=0))
@@ -339,7 +352,8 @@
         halo_copy(off).wait_send()
     for side in range(2):
         held_copy(side).wait_send()
-    all_of(spread_in, n_loc - 1, loc_s, loc_r).wait_send()
+    all_of(spread_in, n_loc // 2 - 1, loc_s, loc_r).wait_send()
+    pair_copy.wait_send()
     all_of(part_in, n_grp - 1, grp_s, grp_r).wait_send()
 
 
@@ -387,14 +401,16 @@
                 pltpu.VMEM((blocks, 256), jnp.int32),
                 pltpu.VMEM((n_loc, 2, listed // chunk, chunk, LANES), F32),
                 pltpu.VMEM((n_loc, 2, listed // chunk, chunk, LANES), F32),
-                pltpu.VMEM((hubs, width), F32),
-                pltpu.VMEM((n_grp, hubs // n_grp, width), F32),
-                pltpu.VMEM((n_loc, padded, width // 2), F32),
-                pltpu.VMEM((n_loc, padded, width // 2), F32),
+                pltpu.VMEM((2, hubs // 2, width), F32),
+                pltpu.VMEM((hubs // 2, width), F32),
+                pltpu.VMEM((n_grp, hubs // n_grp // 2, width), F32),
+                pltpu.VMEM((n_grp, hubs // n_grp // 2, width), F32),
+                pltpu.VMEM((n_loc // 2, padded, width // 2), F32),
+                pltpu.VMEM((n_loc // 2, padded, width // 2), F32),
                 pltpu.VMEM((rows, LANES), F32),
                 pltpu.VMEM(weight.shape, BF),
                 pltpu.VMEM(weight.shape, BF),
-                sem((n_loc,)), sem((n_loc,)), sem, sem, sem, sem,
+                sem((n_loc,)), sem((n_loc,)), sem, sem, sem, sem, sem, sem,
             ],
             compiler_params=pltpu.CompilerParams(
                 collective_id=0, has_side_effects=True, vmem_limit_bytes=48 * 1024 * 1024

time: 19.2 us -> 19 us (0.990)
    pallas_call x1, Pallas kernels: 18 us -> 17.9 us  [on_device(): pl.pallas_call(functools.partial(kernel, n_grp, n_loc), out_shape=jax.Sha...]
where the time goes in v5:
time: 19 us; the launch traced here: 18.8 us
  Pallas kernels  17.9 us (94%)
  local copies, waits for them, and re-layouts  0.97 us (5%)
    pallas_call x1, Pallas kernels, on_device(): pl.pallas_call(functools.partial(kernel, n_grp, n_loc), out_shape=jax.Sha...  17.9 us
    unnamed x1, local copies, waits for them, and re-layouts  0.97 us

profile of v5, /device:TPU:0, one launch (start us, length us, event | category | flops | bytes accessed | tf_op | source)
XLA Modules:
  0.0 18.8 jit_solution(18334126396256803114)
XLA Ops:
  0.0 17.9 %shard_map.82 = f32[1024,256]{1,0:T(8,128)S(1)} custom-call(f32[1024,256]{1,0:T(8,128)} %feat_hbm.1, bf16[128,1024]{1,0:T(8,128)(2,1)} %hub_hbm.1, s32[4]{0:T(128)} %slot_hbm.1, s32[16,1024]{1,0:T(8,128)} %bitcast.4, s32[1,1024]{1,0:T(1,128)} %bitcast.5, s32[1024]{0:T(1024)} %bitcast.6, f32[256,256]{1,0:T(8,128)} %w_hbm.1, f32[1,256]{1,0:T(1,128)} %bitcast.7), custom_call_target="tpu_custom_call" | custom-call | tf_op jit(solution)/shard_map/pallas_call | solution.py:374
  17.9 1.0 %copy.10 = f32[1024,256]{1,0:T(8,128)} copy(f32[1024,256]{1,0:T(8,128)S(1)} %shard_map.82) | data formatting | bytes 2097152

commit v6 on v5

--- a/solution.py
+++ b/solution.py
@@ -364,7 +364,7 @@
         rows, width = features.shape
         slots = neighbours.shape[1]
         listed = halo_send.shape[1]
-        chunk = 32
+        chunk = 64
         hubs = hub_block.shape[0]
         blocks = rows // (256 // slots)
         padded = -(-2 * hub_slot.shape[0] // 8) * 8

time: 19 us -> 18.9 us (level)
  Pallas kernels: 17.9 us -> 17.7 us
where the time goes in v6:
time: 18.9 us; the launch traced here: 18.7 us
  Pallas kernels  17.7 us (94%)
  local copies, waits for them, and re-layouts  0.97 us (5%)
    pallas_call x1, Pallas kernels, on_device(): pl.pallas_call(functools.partial(kernel, n_grp, n_loc), out_shape=jax.Sha...  17.7 us
    unnamed x1, local copies, waits for them, and re-layouts  0.97 us

profile of v6, /device:TPU:0, one launch (start us, length us, event | category | flops | bytes accessed | tf_op | source)
XLA Modules:
  0.0 18.7 jit_solution(15034047959187065469)
XLA Ops:
  0.0 17.7 %shard_map.82 = f32[1024,256]{1,0:T(8,128)S(1)} custom-call(f32[1024,256]{1,0:T(8,128)} %feat_hbm.1, bf16[128,1024]{1,0:T(8,128)(2,1)} %hub_hbm.1, s32[4]{0:T(128)} %slot_hbm.1, s32[16,1024]{1,0:T(8,128)} %bitcast.4, s32[1,1024]{1,0:T(1,128)} %bitcast.5, s32[1024]{0:T(1024)} %bitcast.6, f32[256,256]{1,0:T(8,128)} %w_hbm.1, f32[1,256]{1,0:T(1,128)} %bitcast.7), custom_call_target="tpu_custom_call" | custom-call | tf_op jit(solution)/shard_map/pallas_call | solution.py:374
  17.8 1.0 %copy.10 = f32[1024,256]{1,0:T(8,128)} copy(f32[1024,256]{1,0:T(8,128)S(1)} %shard_map.82) | data formatting | bytes 2097152
